TPU v7x, 32 devices: a whole 2x2x4 slice. The times are simulated.
32 devices in a mesh: groups: 2 (over x), cells: 16 (over z, y, core).
Axes of the slice: x: 2, y: 2, z: 4, core: 2. Of those that a mesh axis runs over, the one named last changes fastest.
Arguments:
- pair_act: bfloat16 [768, 384, 128], P(('groups', 'cells')), parts along dimension 0, may hold values from -6 to 6
- pair_mask: int32 [768, 384], P(('groups', 'cells')), parts along dimension 0, may hold values from 0 to 1, as said below
- chain_ids: int32 [768], P('groups'), parts along dimension 0, may hold values from 0 to 3, never falling along the last dimension, each value on 1 to 192 neighbouring positions
- proj_weight: bfloat16 [128, 256], replicated, may hold values from -0.5 to 0.5
- gate_weight: bfloat16 [128, 128], replicated, may hold values from -0.5 to 0.5
- chain_bias: float32 [2, 128], replicated, may hold values from -4 to 4
- out_weight: bfloat16 [64, 128], replicated, may hold values from -0.75 to 0.75
- out_grad: bfloat16 [768, 384, 128], P(('groups', 'cells')), parts along dimension 0, may hold values from -6 to 6
Outputs:
- pair_grad: bfloat16 [768, 384, 128], P(('groups', 'cells')), parts along dimension 0
- proj_weight_grad: float32 [256, 256], P('groups'), parts along dimension 0
- gate_weight_grad: float32 [256, 128], P('groups'), parts along dimension 0
- out_weight_grad: float32 [128, 128], P('groups'), parts along dimension 0
There are 2 independent parts, one for each index of `groups`. A program takes and returns all parts, laid end to end along the dimension named above; an argument that names none is the same for every part. Nothing has to cross between parts.
Inputs may be any that keep to these rules, and one draw needn't show every extreme that they name: pair_mask[i, j] = valid[i] * valid[j] for a 0 or 1 validity of each residue.
All inputs are finite; a program needn't handle non-finite values.
Results may differ from a plain program's by a relative error of at most 0.012.
Values may be sent and summed in bfloat16 or wider, within the bound.
No kernel may reach another device: no remote copies, remote signals or barrier semaphores. Data moves between devices by JAX's collectives and lax.ppermute only.
A program may use at most 64 MiB of HBM per device.

v0:
```python
import jax
import jax.numpy as jnp
from jax import lax
from jax.sharding import PartitionSpec as P

EPS = 1e-05


def normalize_axis(values, axis):
    center = values - jnp.mean(values, axis=axis, keepdims=True)
    scale = lax.rsqrt(jnp.mean(center * center, axis=axis, keepdims=True) + EPS)
    return (center * scale, scale)


def norm_backward(grad, normed, scale, axis):
    first = jnp.mean(grad, axis=axis, keepdims=True)
    second = jnp.mean(grad * normed, axis=axis, keepdims=True)
    return scale * (grad - first - normed * second)


def local(
    pair_act, pair_mask, chain_ids, proj_weight, gate_weight, chain_bias, out_weight, out_grad
):
    devices = lax.axis_size("cells")
    rows_here = pair_act.shape[0]
    length = pair_act.shape[1]
    width = pair_act.shape[2]
    hidden = out_weight.shape[0]
    halfway = length // 2
    channel_pairs = devices // 2
    per_device = 2 * hidden // devices
    count = rows_here * length
    zfull = pair_act.astype(jnp.float32).reshape(count, width)
    zhat, zscale = normalize_axis(zfull, 1)
    normed = zhat.astype(jnp.bfloat16)
    projected = jnp.einsum("xc,cf->fx", normed, proj_weight, preferred_element_type=jnp.float32)
    keeper = pair_mask.astype(jnp.float32).reshape(1, count)
    values = projected[: 2 * hidden]
    sigma = jax.nn.sigmoid(projected[2 * hidden :])
    factors = (keeper * sigma * values).astype(jnp.bfloat16)
    outgoing = factors.reshape(2, channel_pairs, per_device, rows_here, 2, halfway)
    outgoing = jnp.transpose(outgoing, (1, 4, 0, 2, 3, 5)).reshape(
        devices, 2, per_device, rows_here, halfway
    )
    arrived = lax.all_to_all(outgoing, "cells", split_axis=0, concat_axis=3, tiled=True)
    left_half = arrived[0, 0]
    right_half = arrived[0, 1]
    partial_value = jnp.einsum(
        "cik,cjk->cij", left_half, right_half, preferred_element_type=jnp.float32
    )
    landed = lax.all_to_all(
        partial_value.reshape(per_device, devices, rows_here, length).astype(jnp.bfloat16),
        "cells",
        split_axis=1,
        concat_axis=0,
        tiled=True,
    ).astype(jnp.float32)
    landed = landed.reshape(channel_pairs, 2, per_device, rows_here, length)
    triangle = jnp.sum(landed, axis=1).reshape(hidden, count)
    tri_hat, tri_scale = normalize_axis(triangle, 0)
    tri_low = tri_hat.astype(jnp.bfloat16)
    outputs = jnp.einsum("hx,hc->xc", tri_low, out_weight, preferred_element_type=jnp.float32)
    start = lax.axis_index("cells") * rows_here
    own_chain = lax.dynamic_slice_in_dim(chain_ids, start, rows_here, 0)
    same_chain = (own_chain[:, None] == chain_ids[None, :]).reshape(count, 1)
    logits = jnp.dot(normed, gate_weight, preferred_element_type=jnp.float32)
    logits = logits + jnp.where(same_chain, chain_bias[0][None, :], chain_bias[1][None, :])
    gating = jax.nn.sigmoid(logits)
    upstream = out_grad.reshape(count, width).astype(jnp.float32)
    d_outputs = (upstream * gating).astype(jnp.bfloat16)
    d_logits = (upstream * outputs * gating * (1.0 - gating)).astype(jnp.bfloat16)
    out_term = jnp.einsum("hx,xc->hc", tri_low, d_outputs, preferred_element_type=jnp.float32)
    gate_term = jnp.einsum("xc,xd->cd", normed, d_logits, preferred_element_type=jnp.float32)
    d_hat = jnp.einsum("xc,hc->hx", d_outputs, out_weight, preferred_element_type=jnp.float32)
    d_tri = norm_backward(d_hat, tri_hat, tri_scale, 0).astype(jnp.bfloat16)
    doubled = jnp.broadcast_to(
        d_tri.reshape(channel_pairs, 1, per_device, rows_here, length),
        (channel_pairs, 2, per_device, rows_here, length),
    )
    whole = lax.all_to_all(
        doubled.reshape(devices, per_device, rows_here, length),
        "cells",
        split_axis=0,
        concat_axis=2,
        tiled=True,
    )[0]
    d_left = jnp.einsum("cij,cjk->cik", whole, right_half, preferred_element_type=jnp.float32)
    d_right = jnp.einsum("cij,cik->cjk", whole, left_half, preferred_element_type=jnp.float32)
    d_pair = jnp.stack([d_left, d_right]).astype(jnp.bfloat16)
    returned = lax.all_to_all(
        d_pair.reshape(2, per_device, devices, rows_here, halfway),
        "cells",
        split_axis=2,
        concat_axis=2,
        tiled=True,
    )
    returned = returned.reshape(2, per_device, channel_pairs, 2, rows_here, halfway)
    d_factors = (
        jnp.transpose(returned, (0, 2, 1, 4, 3, 5)).reshape(2 * hidden, count).astype(jnp.float32)
    )
    d_values = d_factors * keeper * sigma
    d_gates = d_factors * keeper * values * sigma * (1.0 - sigma)
    d_proj = jnp.concatenate([d_values, d_gates], axis=0).astype(jnp.bfloat16)
    proj_term = jnp.einsum("xc,fx->cf", normed, d_proj, preferred_element_type=jnp.float32)
    d_normed = jnp.einsum("fx,cf->xc", d_proj, proj_weight, preferred_element_type=jnp.float32)
    d_normed = d_normed + jnp.einsum(
        "xd,cd->xc", d_logits, gate_weight, preferred_element_type=jnp.float32
    )
    pair_grad = (
        norm_backward(d_normed, zhat, zscale, 1)
        .astype(jnp.bfloat16)
        .reshape(rows_here, length, width)
    )
    proj_sum, gate_sum, out_sum = lax.psum((proj_term, gate_term, out_term), "cells")
    factor = 1.0 / length
    return (pair_grad, proj_sum * factor, gate_sum * factor, out_sum * factor)


def solution(mesh):
    placed = (
        P(("groups", "cells"), None, None),
        P(("groups", "cells"), None),
        P("groups"),
        P(),
        P(),
        P(),
        P(),
        P(("groups", "cells"), None, None),
    )
    return jax.shard_map(
        local,
        mesh=mesh,
        in_specs=placed,
        out_specs=(
            P(("groups", "cells"), None, None),
            P("groups", None),
            P("groups", None),
            P("groups", None),
        ),
        check_vma=False,
    )
```

profile of v0, /device:TPU:0, one launch (start us, length us, event | category | flops | bytes accessed | tf_op | source)
XLA Modules:
  0.0 533.3 jit_solution(7304101476079198480)
XLA Ops:
  7.2 2.5 convert_reduce_fusion
  9.7 2.7 multiply_reduce_fusion.1
  12.6 5.0 fusion.12
  17.5 1.4 convolution_bitcast_fusion
  19.0 3.6 copy-done.1
  22.6 2.3 multiply_convert_fusion.3
  24.9 6.0 %reshape.157 = bf16[2,8,8,24,2,192]{5,4,3,2,1,0:T(2,128)(2,1)} reshape(bf16[128,9216]{1,0:T(8,128)(2,1)} %multiply_convert_fusion.3) | data formatting | bytes 4718592 | tf_op jit(solution)/shard_map/reshape | solution.py:41
  30.9 2.5 copy.21
  33.4 76.8 %all_to_all.47 = bf16[16,2,8,24,192]{4,3,2,1,0:T(8,128)(2,1)S(1)} all-to-all(bf16[16,2,8,24,192]{4,3,2,1,0:T(8,128)(2,1)S(1)} %bitcast.95), channel_id=1, replica_groups=mesh['groups'=2,'cells'=16] {'cells'}, dimensions={0} | all-to-all | bytes 4718592 | tf_op jit(solution)/shard_map/all_to_all | solution.py:45
  110.5 1.0 convolution_convert_fusion
  112.2 1.8 copy.25
  114.0 5.4 %all-to-all-start.1 = ((bf16[8,16,24,384]{3,2,0,1:T(8,128)(2,1)}), bf16[8,16,24,384]{3,2,0,1:T(8,128)(2,1)}, u32[]{:S(2)}, u32[]{:S(2)}) async-start(bf16[8,16,24,384]{3,2,0,1:T(8,128)(2,1)} %copy.25), calls=%async_computation.1 | async-start | bytes 4718592 | tf_op jit(solution)/shard_map/all_to_all | solution.py:51
  119.6 6.6 %fusion.7 = (bf16[9216,128]{1,0:T(8,128)(2,1)}, f32[9216,128]{1,0:T(8,128)}) fusion(bf16[24,384,128]{2,1,0:T(8,128)(2,1)} %param.15, f32[128]{0:T(128)S(1)} %get-tuple-element.11, f32[128]{0:T(128)S(1)} %get-tuple-element.10, pred[9216]{0:T(1024)(128)(4,1)S(1)} %eq.23, bf16[9216,128]{1,0:T(8,128)(2,1)} %copy-done.3, bf16[128,128]{1,0:T(8,128)(2,1)S(1)} %copy-done.14), kind=kOutput, calls=%fused_computation.13 | convolution fusion | flops 311427072 | bytes 11839488 | tf_op jit(solution)/shard_map/dot_general | solution.py:66
  126.3 38.7 %all-to-all-done.1 = bf16[8,16,24,384]{3,2,0,1:T(8,128)(2,1)} async-done(((bf16[8,16,24,384]{3,2,0,1:T(8,128)(2,1)}), bf16[8,16,24,384]{3,2,0,1:T(8,128)(2,1)}, u32[]{:S(2)}, u32[]{:S(2)}) %all-to-all-start.1) | async-done | bytes 2359328 | tf_op jit(solution)/shard_map/all_to_all | solution.py:51
  165.0 2.1 convert_reduce_fusion.1
  167.1 2.4 bitcast_reduce_fusion
  169.7 1.8 copy.27
  171.6 4.8 fusion.20
  176.3 1.8 reduce_sum.86
  178.2 2.9 fusion.19
  181.6 65.9 %all_to_all.48 = bf16[16,8,24,384]{3,2,1,0:T(8,128)(2,1)S(1)} all-to-all(bf16[16,8,24,384]{3,2,1,0:T(8,128)(2,1)S(1)} %bitcast.98), channel_id=1, replica_groups=mesh['groups'=2,'cells'=16] {'cells'}, dimensions={0} | all-to-all | bytes 4718592 | tf_op jit(solution)/shard_map/all_to_all | solution.py:80
  247.9 1.5 copy-done.7
  249.4 2.0 convolution_convert_fusion.1
  251.4 2.1 convolution_convert_fusion.2
  253.5 2.5 copy.30
  256.0 2.5 copy.31
  258.5 2.5 pad_maximum_fusion.1
  261.0 2.0 copy.32
  263.1 4.5 all-to-all-start.3
  267.6 2.9 fusion.22
  270.6 105.9 %psum.23 = f32[64,128]{1,0:T(8,128)S(1)} all-reduce(f32[64,128]{1,0:T(8,128)S(1)} %fusion.22), channel_id=1, replica_groups=mesh['groups'=2,'cells'=16] {'cells'}, use_global_device_ids=true, to_apply=%region_11.12 | all-reduce | flops 8192 | bytes 65536 | tf_op jit(solution)/shard_map/psum | solution.py:114
  377.1 5.4 %fusion.5 = bf16[9216,128]{1,0:T(8,128)(2,1)S(1)} fusion(f32[9216,128]{1,0:T(8,128)} %get-tuple-element.13, bf16[64,128]{1,0:T(8,128)(2,1)S(1)} %copy-done.12, bf16[9216,128]{1,0:T(8,128)(2,1)} %bitcast.104, f32[64,9216]{1,0:T(8,128)} %bitcast.89, f32[9216]{0:T(1024)S(1)} %div.42, f32[9216]{0:T(1024)S(1)} %rsqrt.25), kind=kOutput, calls=%fused_computation.9 | convolution fusion | flops 159842304 | bytes 11886592 | tf_op jit(solution)/shard_map/hx,hc->xc/dot_general | solution.py:62
  382.5 1.5 copy-done.8
  384.0 1.4 fusion.28
  385.5 2.2 copy.33
  387.7 3.5 convert_bitcast_fusion
  391.2 9.0 %copy.34 = f32[2,8,8,24,2,192]{5,4,3,2,1,0:T(2,128)} copy(f32[2,8,8,24,2,192]{5,3,4,1,2,0:T(8,128)} %convert_bitcast_fusion) | data formatting | bytes 9437184 | tf_op jit(solution)/shard_map/convert_element_type | solution.py:99
  400.2 9.3 %reshape.164 = f32[128,9216]{1,0:T(8,128)} reshape(f32[2,8,8,24,2,192]{5,4,3,2,1,0:T(2,128)} %copy.34) | data formatting | bytes 9437184 | tf_op jit(solution)/shard_map/convert_element_type | solution.py:99
  409.5 6.3 %multiply_convert_fusion.2 = (bf16[128,9216]{1,0:T(8,128)(2,1)S(1)}, bf16[128,9216]{1,0:T(8,128)(2,1)S(1)}) fusion(f32[128,9216]{1,0:T(8,128)} %reshape.164, f32[9216]{0:T(1024)S(1)} %mul.128, f32[256,9216]{1,0:T(8,128)} %copy-done.1), kind=kLoop, calls=%fused_computation.25 | loop fusion | flops 12976128 | bytes 18911232 | tf_op jit(solution)/shard_map/convert.7
  415.8 1.4 copy-done.10
  417.2 0.8 copy-done.11
  417.9 2.3 fusion.13
  420.3 4.0 fusion.14
  424.3 8.5 %fusion.27 = (f32[9216]{0:T(1024)S(1)}, f32[9216]{0:T(1024)S(1)}, f32[9216,128]{1,0:T(8,128)}) fusion(f32[9216]{0:T(1024)S(1)} %rsqrt.23, f32[9216]{0:T(1024)S(1)} %div.36, bf16[24,384,128]{2,1,0:T(8,128)(2,1)S(1)} %copy-done.2, f32[9216,128]{1,0:T(8,128)S(1)} %fusion.14, bf16[9216,128]{1,0:T(8,128)(2,1)S(1)} %copy-done.9, bf16[128,128]{1,0:T(8,128)(2,1)S(1)} %copy-done.14), kind=kOutput, calls=%fused_computation.67 | convolution fusion | flops 310228992 | bytes 14336000 | tf_op jit(solution)/shard_map/xd,cd->xc/dot_general | solution.py:106
  432.8 11.2 %multiply_convert_fusion = bf16[9216,128]{1,0:T(8,128)(2,1)} fusion(f32[9216,128]{1,0:T(8,128)} %get-tuple-element.16, bf16[24,384,128]{2,1,0:T(8,128)(2,1)S(1)} %copy-done.2, f32[9216]{0:T(1024)S(1)} %broadcast_multiply_fusion.2, f32[9216]{0:T(1024)S(1)} %broadcast_multiply_fusion.3, f32[9216]{0:T(1024)S(1)} %div.36, f32[9216]{0:T(1024)S(1)} %rsqrt.23), kind=kLoop, calls=%fused_computation.22 | loop fusion | flops 9437184 | bytes 9584640 | tf_op jit(solution)/shard_map/convert_element_type | solution.py:111
  444.0 79.5 %all-reduce.3.cloned.1.call-done = (f32[128,256]{1,0:T(8,128)}, f32[128,128]{1,0:T(8,128)}) async-done(((f32[128,256]{1,0:T(8,128)}, f32[128,128]{1,0:T(8,128)}), (f32[128,256]{1,0:T(8,128)}, f32[128,128]{1,0:T(8,128)})) %all-reduce.3.cloned.1.call-update) | async-done | bytes 196624 | tf_op jit(solution)/shard_map/psum | solution.py:114
  523.5 1.6 broadcast_multiply_fusion
  525.0 1.5 broadcast_multiply_fusion.1
  (55 shorter events, 3.1 us)
Async XLA Ops:
  7.2 10.4 %copy-start = (bf16[128,256]{1,0:T(8,128)(2,1)S(1)}, bf16[128,256]{1,0:T(8,128)(2,1)}, u32[]{:S(2)}) copy-start(bf16[128,256]{1,0:T(8,128)(2,1)} %param.11) | copy-start | bytes 196612
  7.2 2.6 copy-start.2
  7.2 5.3 copy-start.13
  17.5 1.4 copy-start.3
  19.0 3.6 copy-start.1
  110.5 1.6 copy-start.6
  114.0 5.4 %copy-start.15 = (s32[384]{0:T(512)S(1)}, s32[384]{0:T(512)}, u32[]{:S(2)}) copy-start(s32[384]{0:T(512)} %param.10) | copy-start | bytes 4612
  114.0 5.6 %copy-start.16 = (f32[2,128]{1,0:T(2,128)S(1)}, f32[2,128]{1,0:T(2,128)}, u32[]{:S(2)}) copy-start(f32[2,128]{1,0:T(2,128)} %param.13) | copy-start | bytes 3076
  114.0 5.6 %copy-start.14 = (bf16[128,128]{1,0:T(8,128)(2,1)S(1)}, bf16[128,128]{1,0:T(8,128)(2,1)}, u32[]{:S(2)}) copy-start(bf16[128,128]{1,0:T(8,128)(2,1)} %param.12) | copy-start | bytes 98308
  114.0 51.0 %all-to-all-start.1 = ((bf16[8,16,24,384]{3,2,0,1:T(8,128)(2,1)}), bf16[8,16,24,384]{3,2,0,1:T(8,128)(2,1)}, u32[]{:S(2)}, u32[]{:S(2)}) async-start(bf16[8,16,24,384]{3,2,0,1:T(8,128)(2,1)} %copy.25), calls=%async_computation.1 | async-start | bytes 4718592 | tf_op jit(solution)/shard_map/all_to_all | solution.py:51
  169.7 1.9 copy-start.12
  247.5 1.9 copy-start.7
  263.1 122.4 %all-to-all-start.3 = ((bf16[2,8,16,24,192]{4,3,1,0,2:T(8,128)(2,1)}), bf16[2,8,16,24,192]{4,3,1,0,2:T(8,128)(2,1)}, u32[]{:S(2)}, u32[]{:S(2)}) async-start(bf16[2,8,16,24,192]{4,3,1,0,2:T(8,128)(2,1)} %copy.32), calls=%async_computation.3 | async-start | bytes 6291456 | tf_op jit(solution)/shard_map/all_to_all | solution.py:90
  267.6 255.9 %all-reduce.3.cloned.1.call-start = ((), (), s32[]{:S(2)}) async-start(), calls=%async_computation.4 | async-start | bytes 393216 | tf_op jit(solution)/shard_map/psum | solution.py:114
  377.1 6.9 %copy-start.4 = (bf16[9216,128]{1,0:T(8,128)(2,1)S(1)}, bf16[9216,128]{1,0:T(8,128)(2,1)}, u32[]{:S(2)}) copy-start(bf16[9216,128]{1,0:T(8,128)(2,1)} %copy-done.3) | copy-start | bytes 7077892
  382.5 1.5 copy-start.8
  409.5 8.5 %copy-start.5 = (bf16[9216,128]{1,0:T(8,128)(2,1)S(1)}, bf16[9216,128]{1,0:T(8,128)(2,1)}, u32[]{:S(2)}) copy-start(bf16[9216,128]{1,0:T(8,128)(2,1)} %copy-done.3) | copy-start | bytes 7077892
  415.8 1.4 copy-start.10
  415.8 2.2 copy-start.11
  420.3 4.0 copy-start.9
Sparse Core Ops, SparseCore 0:
  432.9 90.5 all-reduce.2
where the time goes:
time: 535 us; the launch traced here: 533 us
  blocking collectives  249 us (47%)
  waiting for transfers between devices  118 us (22%)
  local copies, waits for them, and re-layouts  50.5 us (9%)
  other arithmetic  49.2 us (9%)
  matrix products  42.5 us (8%)
  between operations  14.4 us (3%)
  starting transfers between devices  9.93 us (2%)
    psum x1, blocking collectives, local(): lax.psum((proj_term, gate_term, out_term), 'cells')  106 us
    psum x1, waiting for transfers between devices, local(): lax.psum((proj_term, gate_term, out_term), 'cells')  79.5 us
    all_to_all x1, blocking collectives, local(): lax.all_to_all(outgoing, 'cells', split_axis=0, concat_axis=3, tiled=True)  76.8 us
    all_to_all x1, blocking collectives, local(): lax.all_to_all(doubled.reshape(devices, per_device, rows_here, length), '...  65.9 us
    all_to_all x1, waiting for transfers between devices, local(): lax.all_to_all(partial_value.reshape(per_device, devices, rows_here, leng...  38.7 us
    convert_element_type x2, local copies, waits for them, and re-layouts, local(): jnp.transpose(returned, (0, 2, 1, 4, 3, 5)).reshape(2 * hidden, count)  18.3 us
    convert_element_type x1, other arithmetic, local(): pair_grad = norm_backward(d_normed, zhat, zscale, 1).astype(jnp.bfloat16)...  11.2 us
  transfers between devices with their start and end apart: 3, of which 2 were waited for; matrix products, arithmetic and copies ran while one was open for 5% of the time, Pallas kernels for 0%

commit v1 on v0

--- a/solution.py
+++ b/solution.py
@@ -42,7 +42,9 @@
     outgoing = jnp.transpose(outgoing, (1, 4, 0, 2, 3, 5)).reshape(
         devices, 2, per_device, rows_here, halfway
     )
-    arrived = lax.all_to_all(outgoing, "cells", split_axis=0, concat_axis=3, tiled=True)
+    shards = jnp.split(outgoing, lax.axis_size("cells"), axis=0)
+    got = lax.all_to_all(jnp.stack(shards), "cells", 0, 0)
+    arrived = jnp.concatenate(got, axis=3)
     left_half = arrived[0, 0]
     right_half = arrived[0, 1]
     partial_value = jnp.einsum(

time: 535 us -> 536 us (level)
    unnamed x34 -> x49, local copies, waits for them, and re-layouts: 9.5 us -> 10.7 us
where the time goes in v1:
time: 536 us; the launch traced here: 535 us
  blocking collectives  249 us (46%)
  waiting for transfers between devices  118 us (22%)
  local copies, waits for them, and re-layouts  51.7 us (10%)
  other arithmetic  49.2 us (9%)
  matrix products  42.5 us (8%)
  between operations  14.5 us (3%)
  starting transfers between devices  9.93 us (2%)
    psum x1, blocking collectives, local(): lax.psum((proj_term, gate_term, out_term), 'cells')  106 us
    psum x1, waiting for transfers between devices, local(): lax.psum((proj_term, gate_term, out_term), 'cells')  79.5 us
    all_to_all x1, blocking collectives, local(): got = lax.all_to_all(jnp.stack(shards), 'cells', 0, 0)  76.8 us
    all_to_all x1, blocking collectives, local(): lax.all_to_all(doubled.reshape(devices, per_device, rows_here, length), '...  65.9 us
    all_to_all x1, waiting for transfers between devices, local(): lax.all_to_all(partial_value.reshape(per_device, devices, rows_here, leng...  38.7 us
    convert_element_type x2, local copies, waits for them, and re-layouts, local(): jnp.transpose(returned, (0, 2, 1, 4, 3, 5)).reshape(2 * hidden, count)  18.3 us
    convert_element_type x1, other arithmetic, local(): pair_grad = norm_backward(d_normed, zhat, zscale, 1).astype(jnp.bfloat16)...  11.2 us
    unnamed x49, local copies, waits for them, and re-layouts  10.7 us
  transfers between devices with their start and end apart: 3, of which 2 were waited for; matrix products, arithmetic and copies ran while one was open for 5% of the time, Pallas kernels for 0%

profile of v1, /device:TPU:0, one launch (start us, length us, event | category | flops | bytes accessed | tf_op | source)
XLA Modules:
  0.0 534.7 jit_solution(16655016404312911022)
XLA Ops:
  7.2 2.5 convert_reduce_fusion
  9.7 2.7 multiply_reduce_fusion.1
  12.6 5.0 fusion.12
  17.5 1.4 convolution_bitcast_fusion
  19.0 3.6 copy-done.1
  22.6 2.3 multiply_convert_fusion.3
  24.9 6.0 %reshape.163 = bf16[2,8,8,24,2,192]{5,4,3,2,1,0:T(2,128)(2,1)} reshape(bf16[128,9216]{1,0:T(8,128)(2,1)} %multiply_convert_fusion.3) | data formatting | bytes 4718592 | tf_op jit(solution)/shard_map/reshape | solution.py:41
  30.9 2.5 copy.36
  33.7 76.8 %all_to_all.34 = bf16[16,1,2,8,24,192]{5,4,3,2,1,0:T(8,128)(2,1)S(1)} all-to-all(bf16[16,1,2,8,24,192]{5,4,3,2,1,0:T(8,128)(2,1)S(1)} %fusion.25), channel_id=1, replica_groups=mesh['groups'=2,'cells'=16] {'cells'}, dimensions={0} | all-to-all | bytes 4718592 | tf_op jit(solution)/shard_map/all_to_all | solution.py:46
  110.9 1.6 copy-done.6
  112.5 1.0 convolution_convert_fusion
  113.5 1.8 copy.40
  115.3 5.4 %all-to-all-start.1 = ((bf16[8,16,24,384]{3,2,0,1:T(8,128)(2,1)}), bf16[8,16,24,384]{3,2,0,1:T(8,128)(2,1)}, u32[]{:S(2)}, u32[]{:S(2)}) async-start(bf16[8,16,24,384]{3,2,0,1:T(8,128)(2,1)} %copy.40), calls=%async_computation.1 | async-start | bytes 4718592 | tf_op jit(solution)/shard_map/all_to_all | solution.py:53
  121.0 6.6 %fusion.7 = (bf16[9216,128]{1,0:T(8,128)(2,1)}, f32[9216,128]{1,0:T(8,128)}) fusion(bf16[24,384,128]{2,1,0:T(8,128)(2,1)} %param.15, f32[128]{0:T(128)S(1)} %get-tuple-element.11, f32[128]{0:T(128)S(1)} %get-tuple-element.10, pred[9216]{0:T(1024)(128)(4,1)S(1)} %eq.23, bf16[9216,128]{1,0:T(8,128)(2,1)} %copy-done.3, bf16[128,128]{1,0:T(8,128)(2,1)S(1)} %copy-done.14), kind=kOutput, calls=%fused_computation.13 | convolution fusion | flops 311427072 | bytes 11839488 | tf_op jit(solution)/shard_map/dot_general | solution.py:68
  127.6 38.7 %all-to-all-done.1 = bf16[8,16,24,384]{3,2,0,1:T(8,128)(2,1)} async-done(((bf16[8,16,24,384]{3,2,0,1:T(8,128)(2,1)}), bf16[8,16,24,384]{3,2,0,1:T(8,128)(2,1)}, u32[]{:S(2)}, u32[]{:S(2)}) %all-to-all-start.1) | async-done | bytes 2359328 | tf_op jit(solution)/shard_map/all_to_all | solution.py:53
  166.3 2.1 convert_reduce_fusion.1
  168.4 2.4 bitcast_reduce_fusion
  171.1 1.8 copy.42
  172.9 4.8 fusion.20
  177.7 1.8 reduce_sum.86
  179.5 2.9 fusion.19
  183.0 65.9 %all_to_all.35 = bf16[16,8,24,384]{3,2,1,0:T(8,128)(2,1)S(1)} all-to-all(bf16[16,8,24,384]{3,2,1,0:T(8,128)(2,1)S(1)} %bitcast.175), channel_id=1, replica_groups=mesh['groups'=2,'cells'=16] {'cells'}, dimensions={0} | all-to-all | bytes 4718592 | tf_op jit(solution)/shard_map/all_to_all | solution.py:82
  249.2 1.5 copy-done.7
  250.8 2.0 convolution_convert_fusion.1
  252.8 2.1 convolution_convert_fusion.2
  254.9 2.5 copy.45
  257.4 2.5 copy.46
  259.9 2.5 pad_maximum_fusion.1
  262.4 2.0 copy.47
  264.4 4.5 all-to-all-start.3
  269.0 2.9 fusion.22
  271.9 105.9 %psum.23 = f32[64,128]{1,0:T(8,128)S(1)} all-reduce(f32[64,128]{1,0:T(8,128)S(1)} %fusion.22), channel_id=1, replica_groups=mesh['groups'=2,'cells'=16] {'cells'}, use_global_device_ids=true, to_apply=%region_11.12 | all-reduce | flops 8192 | bytes 65536 | tf_op jit(solution)/shard_map/psum | solution.py:116
  378.5 5.4 %fusion.5 = bf16[9216,128]{1,0:T(8,128)(2,1)S(1)} fusion(f32[9216,128]{1,0:T(8,128)} %get-tuple-element.13, bf16[64,128]{1,0:T(8,128)(2,1)S(1)} %copy-done.12, bf16[9216,128]{1,0:T(8,128)(2,1)} %bitcast.181, f32[64,9216]{1,0:T(8,128)} %bitcast.151, f32[9216]{0:T(1024)S(1)} %div.42, f32[9216]{0:T(1024)S(1)} %rsqrt.25), kind=kOutput, calls=%fused_computation.9 | convolution fusion | flops 159842304 | bytes 11886592 | tf_op jit(solution)/shard_map/hx,hc->xc/dot_general | solution.py:64
  383.9 1.5 copy-done.8
  385.4 1.4 fusion.44
  386.8 2.2 copy.48
  389.0 3.5 convert_bitcast_fusion
  392.5 9.0 %copy.49 = f32[2,8,8,24,2,192]{5,4,3,2,1,0:T(2,128)} copy(f32[2,8,8,24,2,192]{5,3,4,1,2,0:T(8,128)} %convert_bitcast_fusion) | data formatting | bytes 9437184 | tf_op jit(solution)/shard_map/convert_element_type | solution.py:101
  401.6 9.3 %reshape.172 = f32[128,9216]{1,0:T(8,128)} reshape(f32[2,8,8,24,2,192]{5,4,3,2,1,0:T(2,128)} %copy.49) | data formatting | bytes 9437184 | tf_op jit(solution)/shard_map/convert_element_type | solution.py:101
  410.8 6.3 %multiply_convert_fusion.2 = (bf16[128,9216]{1,0:T(8,128)(2,1)S(1)}, bf16[128,9216]{1,0:T(8,128)(2,1)S(1)}) fusion(f32[128,9216]{1,0:T(8,128)} %reshape.172, f32[9216]{0:T(1024)S(1)} %mul.128, f32[256,9216]{1,0:T(8,128)} %copy-done.1), kind=kLoop, calls=%fused_computation.25 | loop fusion | flops 12976128 | bytes 18911232 | tf_op jit(solution)/shard_map/convert.7
  417.1 1.4 copy-done.10
  419.3 2.3 fusion.13
  421.6 4.0 fusion.14
  425.6 8.5 %fusion.43 = (f32[9216]{0:T(1024)S(1)}, f32[9216]{0:T(1024)S(1)}, f32[9216,128]{1,0:T(8,128)}) fusion(f32[9216]{0:T(1024)S(1)} %rsqrt.23, f32[9216]{0:T(1024)S(1)} %div.36, bf16[24,384,128]{2,1,0:T(8,128)(2,1)S(1)} %copy-done.2, f32[9216,128]{1,0:T(8,128)S(1)} %fusion.14, bf16[9216,128]{1,0:T(8,128)(2,1)S(1)} %copy-done.9, bf16[128,128]{1,0:T(8,128)(2,1)S(1)} %copy-done.14), kind=kOutput, calls=%fused_computation.99 | convolution fusion | flops 310228992 | bytes 14336000 | tf_op jit(solution)/shard_map/xd,cd->xc/dot_general | solution.py:108
  434.2 11.2 %multiply_convert_fusion = bf16[9216,128]{1,0:T(8,128)(2,1)} fusion(f32[9216,128]{1,0:T(8,128)} %get-tuple-element.16, bf16[24,384,128]{2,1,0:T(8,128)(2,1)S(1)} %copy-done.2, f32[9216]{0:T(1024)S(1)} %broadcast_multiply_fusion.2, f32[9216]{0:T(1024)S(1)} %broadcast_multiply_fusion.3, f32[9216]{0:T(1024)S(1)} %div.36, f32[9216]{0:T(1024)S(1)} %rsqrt.23), kind=kLoop, calls=%fused_computation.22 | loop fusion | flops 9437184 | bytes 9584640 | tf_op jit(solution)/shard_map/convert_element_type | solution.py:113
  445.4 79.5 %all-reduce.3.cloned.1.call-done = (f32[128,256]{1,0:T(8,128)}, f32[128,128]{1,0:T(8,128)}) async-done(((f32[128,256]{1,0:T(8,128)}, f32[128,128]{1,0:T(8,128)}), (f32[128,256]{1,0:T(8,128)}, f32[128,128]{1,0:T(8,128)})) %all-reduce.3.cloned.1.call-update) | async-done | bytes 196624 | tf_op jit(solution)/shard_map/psum | solution.py:116
  524.8 1.6 broadcast_multiply_fusion
  526.4 1.5 broadcast_multiply_fusion.1
  (71 shorter events, 3.5 us)
Async XLA Ops:
  7.2 10.4 %copy-start = (bf16[128,256]{1,0:T(8,128)(2,1)S(1)}, bf16[128,256]{1,0:T(8,128)(2,1)}, u32[]{:S(2)}) copy-start(bf16[128,256]{1,0:T(8,128)(2,1)} %param.11) | copy-start | bytes 196612
  7.2 2.6 copy-start.2
  7.2 5.3 copy-start.13
  17.5 1.4 copy-start.3
  19.0 3.6 copy-start.1
  110.9 1.6 copy-start.6
  115.3 5.4 %copy-start.15 = (s32[384]{0:T(512)S(1)}, s32[384]{0:T(512)}, u32[]{:S(2)}) copy-start(s32[384]{0:T(512)} %param.10) | copy-start | bytes 4612
  115.3 5.6 %copy-start.16 = (f32[2,128]{1,0:T(2,128)S(1)}, f32[2,128]{1,0:T(2,128)}, u32[]{:S(2)}) copy-start(f32[2,128]{1,0:T(2,128)} %param.13) | copy-start | bytes 3076
  115.3 5.6 %copy-start.14 = (bf16[128,128]{1,0:T(8,128)(2,1)S(1)}, bf16[128,128]{1,0:T(8,128)(2,1)}, u32[]{:S(2)}) copy-start(bf16[128,128]{1,0:T(8,128)(2,1)} %param.12) | copy-start | bytes 98308
  115.3 51.0 %all-to-all-start.1 = ((bf16[8,16,24,384]{3,2,0,1:T(8,128)(2,1)}), bf16[8,16,24,384]{3,2,0,1:T(8,128)(2,1)}, u32[]{:S(2)}, u32[]{:S(2)}) async-start(bf16[8,16,24,384]{3,2,0,1:T(8,128)(2,1)} %copy.40), calls=%async_computation.1 | async-start | bytes 4718592 | tf_op jit(solution)/shard_map/all_to_all | solution.py:53
  170.8 2.1 copy-start.12
  248.9 1.9 copy-start.7
  264.4 122.4 %all-to-all-start.3 = ((bf16[2,8,16,24,192]{4,3,1,0,2:T(8,128)(2,1)}), bf16[2,8,16,24,192]{4,3,1,0,2:T(8,128)(2,1)}, u32[]{:S(2)}, u32[]{:S(2)}) async-start(bf16[2,8,16,24,192]{4,3,1,0,2:T(8,128)(2,1)} %copy.47), calls=%async_computation.3 | async-start | bytes 6291456 | tf_op jit(solution)/shard_map/all_to_all | solution.py:92
  268.9 255.9 %all-reduce.3.cloned.1.call-start = ((), (), s32[]{:S(2)}) async-start(), calls=%async_computation.4 | async-start | bytes 393216 | tf_op jit(solution)/shard_map/psum | solution.py:116
  378.5 6.9 %copy-start.4 = (bf16[9216,128]{1,0:T(8,128)(2,1)S(1)}, bf16[9216,128]{1,0:T(8,128)(2,1)}, u32[]{:S(2)}) copy-start(bf16[9216,128]{1,0:T(8,128)(2,1)} %copy-done.3) | copy-start | bytes 7077892
  383.9 1.5 copy-start.8
  410.8 8.5 %copy-start.5 = (bf16[9216,128]{1,0:T(8,128)(2,1)S(1)}, bf16[9216,128]{1,0:T(8,128)(2,1)}, u32[]{:S(2)}) copy-start(bf16[9216,128]{1,0:T(8,128)(2,1)} %copy-done.3) | copy-start | bytes 7077892
  417.1 1.4 copy-start.10
  417.1 2.2 copy-start.11
  421.6 4.0 copy-start.9
Sparse Core Ops, SparseCore 0:
  434.3 90.5 all-reduce.2
